TPU v7x, 128 devices: a whole 4x4x4 slice. The times are simulated.
128 devices in a mesh: grp: 4 (over z), seq: 32 (over x, y, core).
Axes of the slice: x: 4, y: 4, z: 4, core: 2. Of those that a mesh axis runs over, the one named last changes fastest.
Arguments:
- latent: bfloat16 [4, 4096, 32, 256], P('grp', 'seq'), may hold values from -6 to 6
- up_key: bfloat16 [4, 128, 256], replicated, may hold values from -0.5 to 0.5
- up_value: bfloat16 [4, 128, 256], replicated, may hold values from -0.5 to 0.5
- queries: bfloat16 [8, 64, 128], replicated, may hold values from -240 to 240, as said below
- lengths: int32 [8], replicated, may hold values from 1 to 16384
- block_dest: int32 [4096], replicated, may hold values from 0 to 127, as said below
Outputs:
- decode_latent: bfloat16 [128, 4, 32, 32, 256], P(('grp', 'seq'))
- attended: float32 [8, 8192], replicated
Inputs may be any that keep to these rules, and one draw needn't show every extreme that they name: `block_dest`: each aligned run of 128 entries (the blocks of one seq index in the prefill layout) names every decode device exactly once. `queries`: the new token's query entries, real-valued.
All inputs are finite; a program needn't handle non-finite values.
Results may differ from a plain program's by a relative error of at most 0.001.
Values may be sent and summed in bfloat16 or wider, within the bound.
A program may use at most 64 MiB of HBM per device.

v0:
```python
import jax
import jax.numpy as jnp
from jax import lax
from jax.sharding import Mesh
from jax.sharding import PartitionSpec as P

SEQ = ("seq_0", "seq_1", "seq_2")
GRP_SEQ = ("grp", "seq_0", "seq_1", "seq_2")


def all_in_one(x, axis):
    leaves = jax.tree.leaves(x)
    turns = sorted(range(len(leaves)), key=lambda k: -leaves[k].size)
    width = (1, *leaves[turns[0]].shape)[-1]
    lines = [
        jnp.pad(leaves[k].reshape(-1), (0, -leaves[k].size % width)).reshape(-1, width)
        for k in turns
    ]
    both, at, found = (lax.all_gather(jnp.concatenate(lines), axis), 0, {})
    for k, line in zip(turns, lines):
        slab = both[:, at : at + len(line)].reshape(len(both), -1)
        found[k] = slab[:, : leaves[k].size].reshape(-1, *leaves[k].shape)
        at += len(line)
    numbers = iter(range(len(leaves)))
    return jax.tree.map(lambda _: found[next(numbers)], x)


def joined_all(x, axes, combine):
    for axis in axes:
        pieces = all_in_one(x, axis)
        x = jax.tree.map(lambda part: part[0], pieces)
        for k in range(1, lax.axis_size(axis)):
            x = combine(x, jax.tree.map(lambda part: part[k], pieces))
    return x


def combine(first, second):
    largest = jnp.maximum(first[0], second[0])
    factor_a = jnp.exp(first[0] - largest)
    factor_b = jnp.exp(second[0] - largest)
    totals = first[1] * factor_a + second[1] * factor_b
    accum = first[2] * factor_a[..., None] + second[2] * factor_b[..., None]
    return (largest, totals, accum)


def slot_info(global_ids, lengths, block_len, blk_seq, batch):
    seq_ids = global_ids // blk_seq
    starts = global_ids % blk_seq * block_len
    positions = starts[:, None] + jnp.arange(block_len, dtype=jnp.int32)[None, :]
    seq_hot = (seq_ids[:, None] == jnp.arange(batch, dtype=jnp.int32)[None, :]).astype(jnp.int32)
    slot_len = jnp.sum(seq_hot * lengths[None, :], axis=1)
    live = positions < slot_len[:, None]
    return (seq_hot, live)


def partials(cache, key_map, value_map, slot_query, live, seq_hot):
    rank = cache.shape[3] // 2
    head_dim = slot_query.shape[-1]
    scale = 1.0 / float(head_dim) ** 0.5
    highest = lax.Precision.HIGHEST
    key_lat = cache[..., :rank]
    value_lat = cache[..., rank:]
    keys = jnp.einsum("gstr,grkd->gstkd", key_lat, key_map, preferred_element_type=jnp.float32)
    scores = (
        jnp.einsum("gstkd,sgkjd->gskjt", keys, slot_query.astype(jnp.float32), precision=highest)
        * scale
    )
    live_wide = live[None, :, None, None, :]
    scores = jnp.where(live_wide, scores, -1e30)
    slot_max = jnp.max(scores, axis=-1)
    weights = jnp.where(live_wide, jnp.exp(scores - slot_max[..., None]), 0.0)
    slot_tot = jnp.sum(weights, axis=-1)
    values = jnp.einsum(
        "gstr,grkd->gstkd", value_lat, value_map, preferred_element_type=jnp.float32
    )
    slot_acc = jnp.einsum("gskjt,gstkd->gskjd", weights, values, precision=highest)
    hot_bool = seq_hot > 0
    hot_float = seq_hot.astype(jnp.float32)
    spread = jnp.where(hot_bool[None, :, None, None, :], slot_max[..., None], -1e30)
    seq_max = jnp.max(spread, axis=1)
    slot_seq_max = jnp.sum(
        jnp.where(hot_bool[None, :, None, None, :], seq_max[:, None], 0.0), axis=-1
    )
    factor = jnp.exp(slot_max - slot_seq_max)
    totals = jnp.einsum("gskj,sb->gkjb", slot_tot * factor, hot_float, precision=highest)
    accum = jnp.einsum(
        "gskjd,sb->gkjbd", slot_acc * factor[..., None], hot_float, precision=highest
    )
    return (seq_max, totals, accum)


def body(latent, up_key, up_value, queries, lengths, block_dest):
    groups = up_key.shape[0]
    dests = latent.shape[1]
    block_len = latent.shape[2]
    rank = latent.shape[3] // 2
    shards = block_dest.shape[0] // dests
    batch = queries.shape[0]
    q_heads = queries.shape[1]
    head_dim = queries.shape[2]
    per_group = up_key.shape[2] // head_dim
    per_kv = q_heads // (groups * per_group)
    blk_seq = block_dest.shape[0] // batch
    own_shard = lax.axis_index(SEQ)
    own_dests = lax.dynamic_slice_in_dim(block_dest, own_shard * dests, dests)
    source_order = (
        jnp.zeros((dests,), jnp.int32).at[own_dests].set(jnp.arange(dests, dtype=jnp.int32))
    )
    outgoing = latent[0][source_order]
    received = lax.all_to_all(outgoing, GRP_SEQ, split_axis=0, concat_axis=0, tiled=True)
    received = received.reshape(groups, shards, block_len, 2 * rank)
    decode_latent = received[None]
    key_map = up_key.reshape(groups, rank, per_group, head_dim)
    value_map = up_value.reshape(groups, rank, per_group, head_dim)
    query_rows = queries.reshape(batch, q_heads * head_dim)
    own_group = lax.axis_index("grp")
    slots = latent.shape[1]
    global_ids = own_shard * slots + jnp.arange(slots, dtype=jnp.int32)
    seq_hot, live = slot_info(global_ids, lengths, block_len, blk_seq, batch)
    picked = jnp.dot(seq_hot.astype(jnp.bfloat16), query_rows, preferred_element_type=jnp.float32)
    slot_query = picked.astype(jnp.bfloat16).reshape(slots, groups, per_group, per_kv, head_dim)
    group_query = lax.dynamic_slice_in_dim(slot_query, own_group, 1, 1)
    group_key = lax.dynamic_slice_in_dim(key_map, own_group, 1, 0)
    group_value = lax.dynamic_slice_in_dim(value_map, own_group, 1, 0)
    local = partials(latent, group_key, group_value, group_query, live, seq_hot)
    merged = joined_all(local, SEQ, combine)
    part_result = merged[2] / merged[1][..., None]
    result = lax.all_gather(part_result, "grp", axis=0, tiled=True)
    attended = jnp.transpose(result, (3, 0, 1, 2, 4)).reshape(batch, q_heads * head_dim)
    return (decode_latent, attended)


def solution(mesh):
    finer = Mesh(
        mesh.devices.reshape(mesh.shape["grp"], 4, 4, 2), ("grp", "seq_0", "seq_1", "seq_2")
    )
    in_specs = (P("grp", SEQ, None, None), P(), P(), P(), P(), P())
    out_specs = (P(GRP_SEQ, None, None, None, None), P())
    return jax.shard_map(body, mesh=finer, in_specs=in_specs, out_specs=out_specs, check_vma=False)
```

profile of v0, /device:TPU:0, one launch (start us, length us, event | category | flops | bytes accessed | tf_op | source)
XLA Modules:
  0.0 82.2 jit_solution(2277621008148799493)
XLA Ops:
  0.6 0.8 compare_select_fusion.1
  1.4 1.0 %scatter_custom_fusion = s32[128]{0:T(128)S(1)} fusion(s32[128]{0:T(128)S(1)} %compare_select_fusion.1, s32[128]{0:T(128)S(1)} %iota.27, s32[]{:T(128)} %constant.26.clone.1), kind=kCustom, calls=%fused_computation.172 | custom fusion | bytes 516 | tf_op jit(solution)/shard_map/scatter | solution.py:107
  2.4 3.6 %gather_fusion = bf16[128,32,256]{2,1,0:T(8,128)(2,1)} fusion(bf16[128,32,256]{2,1,0:T(8,128)(2,1)} %bitcast.358, s32[1024]{0:T(1024)S(1)} %pad_clamp_fusion), kind=kCustom, calls=%fused_computation | custom fusion | bytes 4194816 | tf_op jit(solution)/shard_map/gather | solution.py:109
  6.0 11.7 %all-to-all-start = ((bf16[128,32,256]{2,1,0:T(8,128)(2,1)}), bf16[128,32,256]{2,1,0:T(8,128)(2,1)}, u32[]{:S(2)}, u32[]{:S(2)}) async-start(bf16[128,32,256]{2,1,0:T(8,128)(2,1)} %gather_fusion), calls=%async_computation | async-start | bytes 4194304 | tf_op jit(solution)/shard_map/all_to_all | solution.py:110
  18.0 0.1 constant_dynamic-slice_fusion
  18.1 0.7 fusion.14
  18.8 0.2 copy-done.3
  19.0 0.7 fusion.4
  19.8 0.6 copy.35
  20.4 0.1 add_compare_fusion
  20.5 3.6 %fusion.102 = (f32[128,2,8]{2,1,0:T(2,128)S(1)}, f32[128,2,8,32]{3,2,1,0:T(8,128)S(1)}) fusion(f32[2,128,128,32]{1,3,0,2:T(8,128)S(1)} %fusion.14, bf16[128,4,2,8,128]{4,3,2,1,0:T(8,128)(2,1)S(1)} %bitcast.359, s32[]{:T(128)S(6)} %select_n.72, pred[128,32]{1,0:T(8,128)(4,1)S(1)} %add_compare_fusion), kind=kOutput, calls=%fused_computation.176 | convolution fusion | flops 100857856 | bytes 5005316 | tf_op jit(solution)/shard_map/gstkd,sgkjd->gskjt/dot_general | solution.py:65
  24.2 0.1 select_reduce_fusion.1
  24.3 0.1 select_reduce_fusion
  24.4 0.1 reshape.1166
  24.5 0.1 copy.26
  24.7 0.7 convolution_bitcast_fusion
  25.4 0.8 fusion.21
  26.2 3.7 %fusion.5 = f32[128,2,8,128]{3,2,1,0:T(8,128)S(1)} fusion(f32[128,32,2,128]{3,1,0,2:T(8,128)S(1)} %convolution_bitcast_fusion, f32[128,2,8,32]{3,2,1,0:T(8,128)S(1)} %get-tuple-element.30, f32[128,2,8]{2,1,0:T(2,128)S(1)} %copy.26, f32[128,2,8]{2,1,0:T(2,128)S(1)} %get-tuple-element.29, pred[128,32]{1,0:T(8,128)(4,1)S(1)} %add_compare_fusion), kind=kOutput, calls=%fused_computation.9 | convolution fusion | flops 101056512 | bytes 5525504 | tf_op jit(solution)/shard_map/gskjt,gstkd->gskjd/dot_general | solution.py:76
  29.9 0.9 %fusion.17 = f32[8,2,8,128]{3,0,2,1:T(8,128)S(1)} fusion(f32[128,2,8,128]{3,2,1,0:T(8,128)S(1)} %fusion.5, s32[128]{0:T(128)S(1)} %get-tuple-element.31), kind=kOutput, calls=%fused_computation.15 | convolution fusion | flops 25168896 | bytes 1114624 | tf_op jit(solution)/shard_map/gskjd,sb->gkjbd/dot_general | solution.py:86
  30.8 0.1 fusion.49
  30.9 0.1 reshape.1167
  31.1 18.3 %all-gather.3 = f32[4,130,128]{2,1,0:T(8,128)S(1)} all-gather(f32[1,130,128]{2,1,0:T(8,128)S(1)} %maximum_bitcast_fusion), channel_id=2, replica_groups=mesh['grp'=4,'seq_0'=4,'seq_1'=4,'seq_2'=2] {'seq_0'}, dimensions={0}, use_global_device_ids=true | all-gather | bytes 332800 | tf_op jit(solution)/shard_map/all_gather | solution.py:19
  49.4 0.2 fusion.39
  49.6 12.7 %all-gather.4 = f32[4,130,128]{2,1,0:T(8,128)S(1)} all-gather(f32[1,130,128]{2,1,0:T(8,128)S(1)} %maximum_bitcast_fusion.1), channel_id=3, replica_groups=mesh['grp'=4,'seq_0'=4,'seq_1'=4,'seq_2'=2] {'seq_1'}, dimensions={0}, use_global_device_ids=true | all-gather | bytes 332800 | tf_op jit(solution)/shard_map/all_gather | solution.py:19
  62.4 0.2 fusion.30
  62.6 1.9 %all-gather.5 = f32[2,130,128]{2,1,0:T(8,128)S(1)} all-gather(f32[1,130,128]{2,1,0:T(8,128)S(1)} %maximum_bitcast_fusion.2), channel_id=4, replica_groups=mesh['grp'=4,'seq_0'=4,'seq_1'=4,'seq_2'=2] {'seq_2'}, dimensions={0}, use_global_device_ids=true | all-gather | bytes 199680 | tf_op jit(solution)/shard_map/all_gather | solution.py:19
  64.7 0.1 squeeze.146
  64.8 0.1 squeeze.147
  64.9 0.1 add_divide_fusion
  65.0 13.4 %all_gather.27 = f32[4,2,8,8,128]{4,3,2,1,0:T(8,128)S(1)} all-gather(f32[1,2,8,8,128]{4,3,2,1,0:T(8,128)S(1)} %add_divide_fusion), channel_id=1, replica_groups=mesh['grp'=4,'seq_0'=4,'seq_1'=4,'seq_2'=2] {'grp'}, dimensions={0}, use_global_device_ids=true | all-gather | bytes 327680 | tf_op jit(solution)/shard_map/all_gather | solution.py:128
  78.4 3.1 %copy.52 = bf16[1,4,32,32,256]{4,3,2,1,0:T(8,128)(2,1)} copy(bf16[1,4,32,32,256]{4,3,2,1,0:T(8,128)(2,1)} %bitcast.1) | data formatting | bytes 4194304
  81.5 0.7 copy.53
  (35 shorter events, 0.7 us)
Async XLA Ops:
  6.0 11.8 %copy-start.4 = (s32[8]{0:T(128)S(1)}, s32[8]{0:T(128)}, u32[]{:S(2)}) copy-start(s32[8]{0:T(128)} %param.10) | copy-start | bytes 100
  6.0 11.9 %copy-start.1 = (bf16[4,128,256]{2,1,0:T(8,128)(2,1)S(1)}, bf16[4,128,256]{2,1,0:T(8,128)(2,1)}, u32[]{:S(2)}) copy-start(bf16[4,128,256]{2,1,0:T(8,128)(2,1)} %param.7) | copy-start | bytes 786436
  6.0 11.9 %copy-start.2 = (bf16[4,128,256]{2,1,0:T(8,128)(2,1)S(1)}, bf16[4,128,256]{2,1,0:T(8,128)(2,1)}, u32[]{:S(2)}) copy-start(bf16[4,128,256]{2,1,0:T(8,128)(2,1)} %param.8) | copy-start | bytes 786436
  6.0 12.1 %copy-start = (bf16[1,128,32,256]{3,2,1,0:T(8,128)(2,1)S(1)}, bf16[1,128,32,256]{3,2,1,0:T(8,128)(2,1)}, u32[]{:S(2)}) copy-start(bf16[1,128,32,256]{3,2,1,0:T(8,128)(2,1)} %param.6) | copy-start | bytes 6291460
  6.0 72.4 %all-to-all-start = ((bf16[128,32,256]{2,1,0:T(8,128)(2,1)}), bf16[128,32,256]{2,1,0:T(8,128)(2,1)}, u32[]{:S(2)}, u32[]{:S(2)}) async-start(bf16[128,32,256]{2,1,0:T(8,128)(2,1)} %gather_fusion), calls=%async_computation | async-start | bytes 4194304 | tf_op jit(solution)/shard_map/all_to_all | solution.py:110
  18.1 0.9 %copy-start.3 = (bf16[8,64,128]{2,1,0:T(8,128)(2,1)S(1)}, bf16[8,64,128]{2,1,0:T(8,128)(2,1)}, u32[]{:S(2)}) copy-start(bf16[8,64,128]{2,1,0:T(8,128)(2,1)} %param.9) | copy-start | bytes 393220
where the time goes:
time: 82.5 us; the launch traced here: 82.2 us
  blocking collectives  46.3 us (56%)
  starting transfers between devices  11.7 us (14%)
  matrix products  10.4 us (13%)
  local copies, waits for them, and re-layouts  10.2 us (12%)
  other arithmetic  2.58 us (3%)
  between operations  0.89 us (1%)
    all_gather x3, blocking collectives, all_in_one(): both, at, found = (lax.all_gather(jnp.concatenate(lines), axis), 0, {})  32.9 us
    all_gather x1, blocking collectives, body(): result = lax.all_gather(part_result, 'grp', axis=0, tiled=True)  13.4 us
    all_to_all x1, starting transfers between devices, body(): lax.all_to_all(outgoing, GRP_SEQ, split_axis=0, concat_axis=0, tiled=True)  11.7 us
    unnamed x13, local copies, waits for them, and re-layouts  4.61 us
    dot_general x1, matrix products, partials(): jnp.einsum('gskjt,gstkd->gskjd', weights, values, precision=highest)  3.68 us
    dot_general x1, matrix products, partials(): jnp.einsum('gstkd,sgkjd->gskjt', keys, slot_query.astype(jnp.float32), pr...  3.63 us
    gather x1, local copies, waits for them, and re-layouts, body(): outgoing = latent[0][source_order]  3.59 us
  transfers between devices with their start and end apart: 1, of which 0 were waited for; matrix products, arithmetic and copies ran while one was open for 17% of the time, Pallas kernels for 0%

commit v1 on v0

--- a/solution.py
+++ b/solution.py
@@ -6,6 +6,12 @@
 
 SEQ = ("seq_0", "seq_1", "seq_2")
 GRP_SEQ = ("grp", "seq_0", "seq_1", "seq_2")
+
+
+def laid_out(pieces, dim):
+    lengths = list(pieces.shape[1:])
+    lengths[dim] *= pieces.shape[0]
+    return jnp.moveaxis(pieces, 0, dim).reshape(lengths)
 
 
 def all_in_one(x, axis):
@@ -125,7 +131,19 @@
     local = partials(latent, group_key, group_value, group_query, live, seq_hot)
     merged = joined_all(local, SEQ, combine)
     part_result = merged[2] / merged[1][..., None]
-    result = lax.all_gather(part_result, "grp", axis=0, tiled=True)
+    length = lax.axis_size("grp")
+    pairs = [(i, (i + 1) % length) for i in range(length)]
+    back = [(b, a) for a, b in pairs]
+    lower, upper = ([], [])
+    for step in range(length - 1):
+        if step % 2 == 0:
+            lower.append(lax.ppermute(lower[-1] if lower else part_result, "grp", pairs))
+        else:
+            upper.append(lax.ppermute(upper[-1] if upper else part_result, "grp", back))
+    blocks = jnp.stack([*lower[::-1], part_result, *upper])
+    shift = lax.axis_index("grp") - len(lower)
+    blocks = blocks[(jnp.arange(length) - shift) % length]
+    result = laid_out(blocks, 0)
     attended = jnp.transpose(result, (3, 0, 1, 2, 4)).reshape(batch, q_heads * head_dim)
     return (decode_latent, attended)
 

time: 82.5 us -> 81.4 us (0.987)
  blocking collectives: 46.3 us -> 32.9 us
  waiting for transfers between devices: 0.01 us -> 7.65 us
  starting transfers between devices: 11.7 us -> 15.6 us
    all_gather x1 -> x0, blocking collectives: 13.4 us -> none  [body(): result = lax.all_gather(part_result, 'grp', axis=0, tiled=True)]
    ppermute x0 -> x3, waiting for transfers between devices: none -> 7.65 us  [the longest x2 7.65 us: body(): lax.ppermute(lower[-1] if lower else part_result, 'grp', pairs)]
    ppermute x0 -> x3, starting transfers between devices: none -> 3.92 us  [the longest x1 2.01 us: body(): upper.append(lax.ppermute(upper[-1] if upper else part_result, 'grp', back))]
    gather x0 -> x1, local copies, waits for them, and re-layouts: none -> 1.27 us  [body(): blocks = blocks[(jnp.arange(length) - shift) % length]]
    unnamed x13 -> x12, local copies, waits for them, and re-layouts: 4.61 us -> 3.91 us
  transfers between devices with their start and end apart: 1 -> 4, of which waited for: 0 -> 2; matrix products, arithmetic and copies ran while one was open for 17% -> 19% of each run, Pallas kernels for 0% -> 0%
where the time goes in v1:
time: 81.4 us; the launch traced here: 81.1 us
  blocking collectives  32.9 us (40%)
  starting transfers between devices  15.6 us (19%)
  local copies, waits for them, and re-layouts  10.8 us (13%)
  matrix products  10.4 us (13%)
  waiting for transfers between devices  7.65 us (9%)
  other arithmetic  2.75 us (3%)
  between operations  0.92 us (1%)
    all_gather x3, blocking collectives, all_in_one(): both, at, found = (lax.all_gather(jnp.concatenate(lines), axis), 0, {})  32.9 us
    all_to_all x1, starting transfers between devices, body(): lax.all_to_all(outgoing, GRP_SEQ, split_axis=0, concat_axis=0, tiled=True)  11.7 us
    ppermute x2, waiting for transfers between devices, body(): lax.ppermute(lower[-1] if lower else part_result, 'grp', pairs)  7.65 us
    unnamed x12, local copies, waits for them, and re-layouts  3.91 us
    dot_general x1, matrix products, partials(): jnp.einsum('gskjt,gstkd->gskjd', weights, values, precision=highest)  3.68 us
    dot_general x1, matrix products, partials(): jnp.einsum('gstkd,sgkjd->gskjt', keys, slot_query.astype(jnp.float32), pr...  3.63 us
    gather x1, local copies, waits for them, and re-layouts, body(): outgoing = latent[0][source_order]  3.59 us
    ppermute x1, starting transfers between devices, body(): upper.append(lax.ppermute(upper[-1] if upper else part_result, 'grp', back))  2.01 us
  transfers between devices with their start and end apart: 4, of which 2 were waited for; matrix products, arithmetic and copies ran while one was open for 19% of the time, Pallas kernels for 0%

profile of v1, /device:TPU:0, one launch (start us, length us, event | category | flops | bytes accessed | tf_op | source)
XLA Modules:
  0.0 81.1 jit_solution(7289924709529206571)
XLA Ops:
  0.6 0.8 compare_select_fusion.2
  1.4 1.0 %scatter_custom_fusion = s32[128]{0:T(128)S(1)} fusion(s32[128]{0:T(128)S(1)} %compare_select_fusion.2, s32[128]{0:T(128)S(1)} %iota.31, s32[]{:T(128)} %constant.63.clone.1), kind=kCustom, calls=%fused_computation.182 | custom fusion | bytes 516 | tf_op jit(solution)/shard_map/scatter | solution.py:113
  2.4 3.6 %gather_fusion = bf16[128,32,256]{2,1,0:T(8,128)(2,1)} fusion(bf16[128,32,256]{2,1,0:T(8,128)(2,1)} %bitcast.367, s32[1024]{0:T(1024)S(1)} %pad_clamp_fusion.1), kind=kCustom, calls=%fused_computation | custom fusion | bytes 4194816 | tf_op jit(solution)/shard_map/gather | solution.py:115
  6.0 11.7 %all-to-all-start = ((bf16[128,32,256]{2,1,0:T(8,128)(2,1)}), bf16[128,32,256]{2,1,0:T(8,128)(2,1)}, u32[]{:S(2)}, u32[]{:S(2)}) async-start(bf16[128,32,256]{2,1,0:T(8,128)(2,1)} %gather_fusion), calls=%async_computation | async-start | bytes 4194304 | tf_op jit(solution)/shard_map/all_to_all | solution.py:116
  18.0 0.1 constant_dynamic-slice_fusion
  18.1 0.7 fusion.14
  18.8 0.2 copy-done.3
  19.0 0.7 fusion.4
  19.8 0.6 copy.35
  20.4 0.1 add_compare_fusion
  20.5 3.6 %fusion.104 = (f32[128,2,8]{2,1,0:T(2,128)S(1)}, f32[128,2,8,32]{3,2,1,0:T(8,128)S(1)}) fusion(f32[2,128,128,32]{1,3,0,2:T(8,128)S(1)} %fusion.14, bf16[128,4,2,8,128]{4,3,2,1,0:T(8,128)(2,1)S(1)} %bitcast.368, s32[]{:T(128)S(6)} %select_n.95, pred[128,32]{1,0:T(8,128)(4,1)S(1)} %add_compare_fusion), kind=kOutput, calls=%fused_computation.186 | convolution fusion | flops 100857856 | bytes 5005316 | tf_op jit(solution)/shard_map/gstkd,sgkjd->gskjt/dot_general | solution.py:71
  24.2 0.1 select_reduce_fusion.1
  24.5 0.1 copy.26
  24.7 0.7 convolution_bitcast_fusion
  25.4 0.8 fusion.21
  26.2 3.7 %fusion.5 = f32[128,2,8,128]{3,2,1,0:T(8,128)S(1)} fusion(f32[128,32,2,128]{3,1,0,2:T(8,128)S(1)} %convolution_bitcast_fusion, f32[128,2,8,32]{3,2,1,0:T(8,128)S(1)} %get-tuple-element.30, f32[128,2,8]{2,1,0:T(2,128)S(1)} %copy.26, f32[128,2,8]{2,1,0:T(2,128)S(1)} %get-tuple-element.29, pred[128,32]{1,0:T(8,128)(4,1)S(1)} %add_compare_fusion), kind=kOutput, calls=%fused_computation.10 | convolution fusion | flops 101056512 | bytes 5525504 | tf_op jit(solution)/shard_map/gskjt,gstkd->gskjd/dot_general | solution.py:82
  29.9 0.9 %fusion.17 = f32[8,2,8,128]{3,0,2,1:T(8,128)S(1)} fusion(f32[128,2,8,128]{3,2,1,0:T(8,128)S(1)} %fusion.5, s32[128]{0:T(128)S(1)} %get-tuple-element.31), kind=kOutput, calls=%fused_computation.16 | convolution fusion | flops 25168896 | bytes 1114624 | tf_op jit(solution)/shard_map/gskjd,sb->gkjbd/dot_general | solution.py:92
  30.8 0.1 fusion.49
  30.9 0.1 reshape.1245
  31.1 18.3 %all-gather.3 = f32[4,130,128]{2,1,0:T(8,128)S(1)} all-gather(f32[1,130,128]{2,1,0:T(8,128)S(1)} %maximum_bitcast_fusion.1), channel_id=2, replica_groups=mesh['grp'=4,'seq_0'=4,'seq_1'=4,'seq_2'=2] {'seq_0'}, dimensions={0}, use_global_device_ids=true | all-gather | bytes 332800 | tf_op jit(solution)/shard_map/all_gather | solution.py:25
  49.4 0.2 fusion.39
  49.6 12.7 %all-gather.4 = f32[4,130,128]{2,1,0:T(8,128)S(1)} all-gather(f32[1,130,128]{2,1,0:T(8,128)S(1)} %maximum_bitcast_fusion.2), channel_id=3, replica_groups=mesh['grp'=4,'seq_0'=4,'seq_1'=4,'seq_2'=2] {'seq_1'}, dimensions={0}, use_global_device_ids=true | all-gather | bytes 332800 | tf_op jit(solution)/shard_map/all_gather | solution.py:25
  62.4 0.2 fusion.30
  62.6 1.9 %all-gather.5 = f32[2,130,128]{2,1,0:T(8,128)S(1)} all-gather(f32[1,130,128]{2,1,0:T(8,128)S(1)} %maximum_bitcast_fusion.3), channel_id=4, replica_groups=mesh['grp'=4,'seq_0'=4,'seq_1'=4,'seq_2'=2] {'seq_2'}, dimensions={0}, use_global_device_ids=true | all-gather | bytes 199680 | tf_op jit(solution)/shard_map/all_gather | solution.py:25
  64.9 0.1 add_divide_fusion.1
  65.0 1.9 %collective-permute-start = (f32[1,2,8,8,128]{4,3,2,1,0:T(8,128)S(1)}, f32[1,2,8,8,128]{4,3,2,1,0:T(8,128)S(1)}, u32[]{:S(2)}, u32[]{:S(2)}) collective-permute-start(f32[1,2,8,8,128]{4,3,2,1,0:T(8,128)S(1)} %add_divide_fusion.1), channel_id=1, source_target_pairs={{0,32},{32,64},{64,96},{96,0},{1,33},{33,65},{65,97},{97,1},{2,34}... | collective-permute-start | bytes 196616 | tf_op jit(solution)/shard_map/ppermute | solution.py:140
  66.9 2.0 %collective-permute-start.2 = (f32[1,2,8,8,128]{4,3,2,1,0:T(8,128)S(1)}, f32[1,2,8,8,128]{4,3,2,1,0:T(8,128)S(1)}, u32[]{:S(2)}, u32[]{:S(2)}) collective-permute-start(f32[1,2,8,8,128]{4,3,2,1,0:T(8,128)S(1)} %add_divide_fusion.1), channel_id=1, source_target_pairs={{32,0},{64,32},{96,64},{0,96},{33,1},{65,33},{97,65},{1,97},{34,2}... | collective-permute-start | bytes 196616 | tf_op jit(solution)/shard_map/ppermute | solution.py:142
  68.9 0.1 add_divide_fusion
  69.1 2.2 %collective-permute-done = f32[1,2,8,8,128]{4,3,2,1,0:T(8,128)S(1)} collective-permute-done((f32[1,2,8,8,128]{4,3,2,1,0:T(8,128)S(1)}, f32[1,2,8,8,128]{4,3,2,1,0:T(8,128)S(1)}, u32[]{:S(2)}, u32[]{:S(2)}) %collective-permute-start) | collective-permute-done | bytes 65568 | tf_op jit(solution)/shard_map/ppermute | solution.py:140
  71.3 5.5 %collective-permute-done.1 = f32[1,2,8,8,128]{4,3,2,1,0:T(8,128)S(1)} collective-permute-done((f32[1,2,8,8,128]{4,3,2,1,0:T(8,128)S(1)}, f32[1,2,8,8,128]{4,3,2,1,0:T(8,128)S(1)}, u32[]{:S(2)}, u32[]{:S(2)}) %collective-permute-start.1) | collective-permute-done | bytes 65568 | tf_op jit(solution)/shard_map/ppermute | solution.py:140
  76.8 1.3 %gather_fusion.1 = f32[4,2,8,8,128]{4,3,2,1,0:T(8,128)} fusion(f32[4,2,8,8,128]{4,3,2,1,0:T(8,128)S(1)} %maximum_bitcast_fusion, s32[1024]{0:T(1024)S(1)} %pad_clamp_fusion), kind=kCustom, calls=%fused_computation.1 | custom fusion | bytes 524304 | tf_op jit(solution)/shard_map/gather | solution.py:145
  78.0 3.1 %copy.51 = bf16[1,4,32,32,256]{4,3,2,1,0:T(8,128)(2,1)} copy(bf16[1,4,32,32,256]{4,3,2,1,0:T(8,128)(2,1)} %bitcast.1) | data formatting | bytes 4194304
  (44 shorter events, 1.1 us)
Async XLA Ops:
  6.0 11.8 %copy-start.4 = (s32[8]{0:T(128)S(1)}, s32[8]{0:T(128)}, u32[]{:S(2)}) copy-start(s32[8]{0:T(128)} %param.10) | copy-start | bytes 100
  6.0 11.9 %copy-start.1 = (bf16[4,128,256]{2,1,0:T(8,128)(2,1)S(1)}, bf16[4,128,256]{2,1,0:T(8,128)(2,1)}, u32[]{:S(2)}) copy-start(bf16[4,128,256]{2,1,0:T(8,128)(2,1)} %param.7) | copy-start | bytes 786436
  6.0 11.9 %copy-start.2 = (bf16[4,128,256]{2,1,0:T(8,128)(2,1)S(1)}, bf16[4,128,256]{2,1,0:T(8,128)(2,1)}, u32[]{:S(2)}) copy-start(bf16[4,128,256]{2,1,0:T(8,128)(2,1)} %param.8) | copy-start | bytes 786436
  6.0 12.1 %copy-start = (bf16[1,128,32,256]{3,2,1,0:T(8,128)(2,1)S(1)}, bf16[1,128,32,256]{3,2,1,0:T(8,128)(2,1)}, u32[]{:S(2)}) copy-start(bf16[1,128,32,256]{3,2,1,0:T(8,128)(2,1)} %param.6) | copy-start | bytes 6291460
  6.0 72.0 %all-to-all-start = ((bf16[128,32,256]{2,1,0:T(8,128)(2,1)}), bf16[128,32,256]{2,1,0:T(8,128)(2,1)}, u32[]{:S(2)}, u32[]{:S(2)}) async-start(bf16[128,32,256]{2,1,0:T(8,128)(2,1)} %gather_fusion), calls=%async_computation | async-start | bytes 4194304 | tf_op jit(solution)/shard_map/all_to_all | solution.py:116
  18.1 0.9 %copy-start.3 = (bf16[8,64,128]{2,1,0:T(8,128)(2,1)S(1)}, bf16[8,64,128]{2,1,0:T(8,128)(2,1)}, u32[]{:S(2)}) copy-start(bf16[8,64,128]{2,1,0:T(8,128)(2,1)} %param.9) | copy-start | bytes 393220
  65.0 6.3 %collective-permute-start = (f32[1,2,8,8,128]{4,3,2,1,0:T(8,128)S(1)}, f32[1,2,8,8,128]{4,3,2,1,0:T(8,128)S(1)}, u32[]{:S(2)}, u32[]{:S(2)}) collective-permute-start(f32[1,2,8,8,128]{4,3,2,1,0:T(8,128)S(1)} %add_divide_fusion.1), channel_id=1, source_target_pairs={{0,32},{32,64},{64,96},{96,0},{1,33},{33,65},{65,97},{97,1},{2,34}... | collective-permute-start | bytes 196616 | tf_op jit(solution)/shard_map/ppermute | solution.py:140
  66.9 4.4 %collective-permute-start.2 = (f32[1,2,8,8,128]{4,3,2,1,0:T(8,128)S(1)}, f32[1,2,8,8,128]{4,3,2,1,0:T(8,128)S(1)}, u32[]{:S(2)}, u32[]{:S(2)}) collective-permute-start(f32[1,2,8,8,128]{4,3,2,1,0:T(8,128)S(1)} %add_divide_fusion.1), channel_id=1, source_target_pairs={{32,0},{64,32},{96,64},{0,96},{33,1},{65,33},{97,65},{1,97},{34,2}... | collective-permute-start | bytes 196616 | tf_op jit(solution)/shard_map/ppermute | solution.py:142
  71.3 5.5 %collective-permute-start.1 = (f32[1,2,8,8,128]{4,3,2,1,0:T(8,128)S(1)}, f32[1,2,8,8,128]{4,3,2,1,0:T(8,128)S(1)}, u32[]{:S(2)}, u32[]{:S(2)}) collective-permute-start(f32[1,2,8,8,128]{4,3,2,1,0:T(8,128)S(1)} %collective-permute-done), channel_id=1, source_target_pairs={{0,32},{32,64},{64,96},{96,0},{1,33},{33,65},{65,97},{97,1},{2,34}... | collective-permute-start | bytes 196616 | tf_op jit(solution)/shard_map/ppermute | solution.py:140
